TPU v7x, 32 devices: a whole 2x2x4 slice. The times are simulated.
32 devices in a mesh: row: 4 (over z), col: 8 (over y, x, core).
Axes of the slice: x: 2, y: 2, z: 4, core: 2. Of those that a mesh axis runs over, the one named last changes fastest.
Arguments:
- rhs: float32 [64, 131072], P(None, ('row', 'col')), may hold values from -6 to 6
- pivots: int32 [4096], replicated, may hold values from 0 to 131071, as said below
- factor: float32 [4096, 4, 8, 128], P('row', None, 'col'), as said below
- diag_inv: float32 [8, 512, 512], P('row'), as said below
Outputs:
- solution: float32 [64, 4, 8, 128], P(None, None, 'col')
Inputs may be any that keep to these rules, and one draw needn't show every extreme that they name: `pivots`: distinct column numbers, the first 4096 entries of a permutation of 0 .. 131071. `factor`: entry (row i, column q) is zero where q >= 512 * (i // 512). `diag_inv`: each block is unit lower triangular.
All inputs are finite; a program needn't handle non-finite values.
Results may differ from a plain program's by a relative error of at most 0.0001.
Values sent between devices are 32-bit elements; how exact they have to be, the bound alone decides.
A program may use at most 64 MiB of HBM per device.

v0:
```python
import jax
import jax.numpy as jnp
from jax import lax
from jax.sharding import PartitionSpec as P


def broadcast(shard, axis, root):
    mine = lax.axis_index(axis) == root
    return lax.psum(jnp.where(mine, shard, jnp.zeros_like(shard)), axis)


def apply_inverse(values, block_inv):
    return lax.dot_general(
        values,
        block_inv,
        (((1,), (1,)), ((), ())),
        precision=lax.Precision.HIGHEST,
        preferred_element_type=jnp.float32,
    )


def per_device(rhs, pivots, factor, diag_inv):
    my_row = lax.axis_index("row")
    my_col = lax.axis_index("col")
    col_count = lax.axis_size("col")
    rhs_count = rhs.shape[0]
    slab_rows = factor.shape[0]
    rounds = factor.shape[1]
    piece_len = factor.shape[3]
    block_len = diag_inv.shape[1]
    pieces = block_len // piece_len
    blocks_here = slab_rows // block_len
    total_blocks = blocks_here * lax.axis_size("row")
    first_column = (my_row * col_count + my_col) * rhs.shape[1]
    source_len = rhs.shape[1]
    located = pivots - first_column
    inside = (located >= 0) & (located < source_len)
    taken = jnp.take(rhs, jnp.clip(located, 0, source_len - 1), axis=1)
    taken = jnp.where(inside[None, :], taken, 0.0)
    permuted = lax.psum_scatter(
        jnp.transpose(
            taken.reshape(rhs_count, blocks_here * lax.axis_size("row"), block_len), (1, 0, 2)
        ),
        "row",
        scatter_dimension=0,
        tiled=True,
    )
    permuted = lax.psum(permuted, "col")
    factor_rows = factor.reshape(slab_rows, rounds * piece_len)

    def advance(number, solved):
        owner_row = number // blocks_here
        local_block = number % blocks_here
        block_rows = lax.dynamic_slice_in_dim(factor_rows, local_block * block_len, block_len, 0)
        partial_value = lax.dot_general(
            solved.reshape(rhs_count, rounds * piece_len),
            block_rows,
            (((1,), (1,)), ((), ())),
            precision=lax.Precision.HIGHEST,
            preferred_element_type=jnp.float32,
        )
        own_rhs = lax.dynamic_index_in_dim(permuted, local_block, 0, keepdims=False)
        block_inv = lax.dynamic_index_in_dim(diag_inv, local_block, 0, keepdims=False)
        summed = lax.psum(partial_value, "col")
        fresh = apply_inverse(own_rhs - summed, block_inv)
        fresh = broadcast(fresh, "row", owner_row)
        first_piece = number * pieces
        offset_piece = (my_col - first_piece) % col_count
        owns = offset_piece < pieces
        which = jnp.clip(offset_piece, 0, pieces - 1)
        local_round = jnp.clip((first_piece + offset_piece) // col_count, 0, rounds - 1)
        piece = lax.dynamic_slice_in_dim(fresh, which * piece_len, piece_len, 1)
        updated = lax.dynamic_update_index_in_dim(solved, piece[:, None, :], local_round, 1)
        return jnp.where(owns, updated, solved)

    start_state = jnp.zeros((rhs_count, rounds, 1, piece_len), jnp.float32)
    return lax.fori_loop(0, total_blocks, advance, start_state)


def solution(mesh):
    return jax.shard_map(
        per_device,
        mesh=mesh,
        in_specs=(P(None, ("row", "col")), P(), P("row", None, "col", None), P("row", None, None)),
        out_specs=P(None, None, "col", None),
        check_vma=False,
    )
```

profile of v0, /device:TPU:0, one launch (start us, length us, event | category | flops | bytes accessed | tf_op | source)
XLA Modules:
  0.0 882.2 jit_solution(17491685887215917001)
XLA Ops:
  8.1 1.8 copy.8
  9.9 14.1 %gather_fusion = f32[4096,64]{1,0:T(8,128)} fusion(f32[64,4096]{0,1:T(8,128)S(1)} %copy.8, s32[4096]{0:T(1024)S(1)} %fusion.8), kind=kCustom, calls=%fused_computation | custom fusion | bytes 2113536 | tf_op jit(solution)/shard_map/jit(_take)/gather | solution.py:38
  24.0 2.2 copy.9
  27.4 30.1 %reduce-scatter.2.cloned.1.call-done = f32[2,64,512]{2,1,0:T(8,128)} async-done(((f32[8,64,512]{2,1,0:T(8,128)}), f32[2,64,512]{2,1,0:T(8,128)}) %reduce-scatter.2.cloned.1.call-update) | async-done | bytes 262160 | tf_op jit(solution)/shard_map/reduce_scatter | solution.py:40
  59.3 53.7 %all-reduce.4.cloned.1.call-done = f32[2,64,512]{2,1,0:T(8,128)} async-done(((f32[2,64,512]{2,1,0:T(8,128)}), f32[2,64,512]{2,1,0:T(8,128)}) %all-reduce.4.cloned.1.call-update) | async-done | bytes 262160 | tf_op jit(solution)/shard_map/psum | solution.py:48
  113.0 761.7 %while.16 = (s32[]{:T(128)}, f32[64,4,1,128]{3,1,0,2:T(4,128)S(1)}, s32[]{:T(128)}, f32[2,64,512]{2,1,0:T(8,128)}, f32[1024,512]{1,0:T(8,128)S(1)}, /*index=5*/f...) while((s32[]{:T(128)}, f32[64,4,1,128]{3,1,0,2:T(4,128)S(1)}, ...), condition=%wide.region_5.6_spmd, body=%wide.region_2.5_spmd.sunk | while | flops 402792448 | bytes 4557184 | solution.py:77
  115.0 54.8 %all-reduce.6.cloned.1.call-done = f32[64,512]{1,0:T(8,128)} async-done(((f32[64,512]{1,0:T(8,128)}), f32[64,512]{1,0:T(8,128)}) %all-reduce.6.cloned.1.call-update) | async-done | bytes 131088 | tf_op jit(solution)/shard_map/while/body/eval_jaxpr/psum | solution.py:64
  169.7 3.1 convolution_select_fusion.2
  172.9 34.1 %all-reduce.8.cloned.1.call-done = f32[64,512]{1,0:T(8,128)} async-done(((f32[64,512]{1,0:T(8,128)}), f32[64,512]{1,0:T(8,128)}) %all-reduce.8.cloned.1.call-update) | async-done | bytes 131088 | tf_op jit(solution)/shard_map/while/body/eval_jaxpr/psum | solution.py:9
  208.1 1.8 convolution_bitcast_fusion.2
  210.0 54.8 %all-reduce.6.cloned.1.call-done = f32[64,512]{1,0:T(8,128)} async-done(((f32[64,512]{1,0:T(8,128)}), f32[64,512]{1,0:T(8,128)}) %all-reduce.6.cloned.1.call-update) | async-done | bytes 131088 | tf_op jit(solution)/shard_map/while/body/eval_jaxpr/psum | solution.py:64
  264.8 3.1 convolution_select_fusion.2
  268.0 34.1 %all-reduce.8.cloned.1.call-done = f32[64,512]{1,0:T(8,128)} async-done(((f32[64,512]{1,0:T(8,128)}), f32[64,512]{1,0:T(8,128)}) %all-reduce.8.cloned.1.call-update) | async-done | bytes 131088 | tf_op jit(solution)/shard_map/while/body/eval_jaxpr/psum | solution.py:9
  305.1 55.1 %all-reduce.6.cloned.1.call-done = f32[64,512]{1,0:T(8,128)} async-done(((f32[64,512]{1,0:T(8,128)}), f32[64,512]{1,0:T(8,128)}) %all-reduce.6.cloned.1.call-update) | async-done | bytes 131088 | tf_op jit(solution)/shard_map/while/body/eval_jaxpr/psum | solution.py:64
  360.1 3.1 convolution_select_fusion.2
  363.3 34.1 %all-reduce.8.cloned.1.call-done = f32[64,512]{1,0:T(8,128)} async-done(((f32[64,512]{1,0:T(8,128)}), f32[64,512]{1,0:T(8,128)}) %all-reduce.8.cloned.1.call-update) | async-done | bytes 131088 | tf_op jit(solution)/shard_map/while/body/eval_jaxpr/psum | solution.py:9
  400.4 55.1 %all-reduce.6.cloned.1.call-done = f32[64,512]{1,0:T(8,128)} async-done(((f32[64,512]{1,0:T(8,128)}), f32[64,512]{1,0:T(8,128)}) %all-reduce.6.cloned.1.call-update) | async-done | bytes 131088 | tf_op jit(solution)/shard_map/while/body/eval_jaxpr/psum | solution.py:64
  455.5 3.1 convolution_select_fusion.2
  458.7 34.1 %all-reduce.8.cloned.1.call-done = f32[64,512]{1,0:T(8,128)} async-done(((f32[64,512]{1,0:T(8,128)}), f32[64,512]{1,0:T(8,128)}) %all-reduce.8.cloned.1.call-update) | async-done | bytes 131088 | tf_op jit(solution)/shard_map/while/body/eval_jaxpr/psum | solution.py:9
  495.8 55.1 %all-reduce.6.cloned.1.call-done = f32[64,512]{1,0:T(8,128)} async-done(((f32[64,512]{1,0:T(8,128)}), f32[64,512]{1,0:T(8,128)}) %all-reduce.6.cloned.1.call-update) | async-done | bytes 131088 | tf_op jit(solution)/shard_map/while/body/eval_jaxpr/psum | solution.py:64
  550.9 3.1 convolution_select_fusion.2
  554.1 34.1 %all-reduce.8.cloned.1.call-done = f32[64,512]{1,0:T(8,128)} async-done(((f32[64,512]{1,0:T(8,128)}), f32[64,512]{1,0:T(8,128)}) %all-reduce.8.cloned.1.call-update) | async-done | bytes 131088 | tf_op jit(solution)/shard_map/while/body/eval_jaxpr/psum | solution.py:9
  589.3 1.8 convolution_bitcast_fusion.2
  591.1 55.1 %all-reduce.6.cloned.1.call-done = f32[64,512]{1,0:T(8,128)} async-done(((f32[64,512]{1,0:T(8,128)}), f32[64,512]{1,0:T(8,128)}) %all-reduce.6.cloned.1.call-update) | async-done | bytes 131088 | tf_op jit(solution)/shard_map/while/body/eval_jaxpr/psum | solution.py:64
  646.2 3.1 convolution_select_fusion.2
  649.4 34.1 %all-reduce.8.cloned.1.call-done = f32[64,512]{1,0:T(8,128)} async-done(((f32[64,512]{1,0:T(8,128)}), f32[64,512]{1,0:T(8,128)}) %all-reduce.8.cloned.1.call-update) | async-done | bytes 131088 | tf_op jit(solution)/shard_map/while/body/eval_jaxpr/psum | solution.py:9
  686.5 54.8 %all-reduce.6.cloned.1.call-done = f32[64,512]{1,0:T(8,128)} async-done(((f32[64,512]{1,0:T(8,128)}), f32[64,512]{1,0:T(8,128)}) %all-reduce.6.cloned.1.call-update) | async-done | bytes 131088 | tf_op jit(solution)/shard_map/while/body/eval_jaxpr/psum | solution.py:64
  741.3 3.1 convolution_select_fusion.2
  744.5 34.1 %all-reduce.8.cloned.1.call-done = f32[64,512]{1,0:T(8,128)} async-done(((f32[64,512]{1,0:T(8,128)}), f32[64,512]{1,0:T(8,128)}) %all-reduce.8.cloned.1.call-update) | async-done | bytes 131088 | tf_op jit(solution)/shard_map/while/body/eval_jaxpr/psum | solution.py:9
  781.6 54.8 %all-reduce.6.cloned.1.call-done = f32[64,512]{1,0:T(8,128)} async-done(((f32[64,512]{1,0:T(8,128)}), f32[64,512]{1,0:T(8,128)}) %all-reduce.6.cloned.1.call-update) | async-done | bytes 131088 | tf_op jit(solution)/shard_map/while/body/eval_jaxpr/psum | solution.py:64
  836.3 3.1 convolution_select_fusion.2
  839.5 34.1 %all-reduce.8.cloned.1.call-done = f32[64,512]{1,0:T(8,128)} async-done(((f32[64,512]{1,0:T(8,128)}), f32[64,512]{1,0:T(8,128)}) %all-reduce.8.cloned.1.call-update) | async-done | bytes 131088 | tf_op jit(solution)/shard_map/while/body/eval_jaxpr/psum | solution.py:9
  (75 shorter events, 24.8 us)
Async XLA Ops:
  6.5 51.0 %reduce-scatter.2.cloned.1.call-start = ((), (), s32[]{:S(2)}) async-start(), calls=%async_computation.1 | async-start | bytes 1310720 | tf_op jit(solution)/shard_map/reduce_scatter | solution.py:40
  27.3 85.6 %all-reduce.4.cloned.1.call-start = ((), (), s32[]{:S(2)}) async-start(), calls=%async_computation.2 | async-start | bytes 524288 | tf_op jit(solution)/shard_map/psum | solution.py:48
  113.0 56.7 %all-reduce.6.cloned.1.call-start = ((), (), s32[]{:S(2)}) async-start(), calls=%async_computation.3 | async-start | bytes 262144 | tf_op jit(solution)/shard_map/while/body/eval_jaxpr/psum | solution.py:64
  114.9 92.2 %all-reduce.8.cloned.1.call-start = ((), (), s32[]{:S(2)}) async-start(), calls=%async_computation.4 | async-start | bytes 262144 | tf_op jit(solution)/shard_map/while/body/eval_jaxpr/psum | solution.py:9
  208.1 56.7 %all-reduce.6.cloned.1.call-start = ((), (), s32[]{:S(2)}) async-start(), calls=%async_computation.3 | async-start | bytes 262144 | tf_op jit(solution)/shard_map/while/body/eval_jaxpr/psum | solution.py:64
  209.9 92.2 %all-reduce.8.cloned.1.call-start = ((), (), s32[]{:S(2)}) async-start(), calls=%async_computation.4 | async-start | bytes 262144 | tf_op jit(solution)/shard_map/while/body/eval_jaxpr/psum | solution.py:9
  303.1 57.0 %all-reduce.6.cloned.1.call-start = ((), (), s32[]{:S(2)}) async-start(), calls=%async_computation.3 | async-start | bytes 262144 | tf_op jit(solution)/shard_map/while/body/eval_jaxpr/psum | solution.py:64
  305.0 92.5 %all-reduce.8.cloned.1.call-start = ((), (), s32[]{:S(2)}) async-start(), calls=%async_computation.4 | async-start | bytes 262144 | tf_op jit(solution)/shard_map/while/body/eval_jaxpr/psum | solution.py:9
  398.5 57.0 %all-reduce.6.cloned.1.call-start = ((), (), s32[]{:S(2)}) async-start(), calls=%async_computation.3 | async-start | bytes 262144 | tf_op jit(solution)/shard_map/while/body/eval_jaxpr/psum | solution.py:64
  400.4 92.5 %all-reduce.8.cloned.1.call-start = ((), (), s32[]{:S(2)}) async-start(), calls=%async_computation.4 | async-start | bytes 262144 | tf_op jit(solution)/shard_map/while/body/eval_jaxpr/psum | solution.py:9
  493.8 57.0 %all-reduce.6.cloned.1.call-start = ((), (), s32[]{:S(2)}) async-start(), calls=%async_computation.3 | async-start | bytes 262144 | tf_op jit(solution)/shard_map/while/body/eval_jaxpr/psum | solution.py:64
  495.7 92.5 %all-reduce.8.cloned.1.call-start = ((), (), s32[]{:S(2)}) async-start(), calls=%async_computation.4 | async-start | bytes 262144 | tf_op jit(solution)/shard_map/while/body/eval_jaxpr/psum | solution.py:9
  589.2 57.0 %all-reduce.6.cloned.1.call-start = ((), (), s32[]{:S(2)}) async-start(), calls=%async_computation.3 | async-start | bytes 262144 | tf_op jit(solution)/shard_map/while/body/eval_jaxpr/psum | solution.py:64
  591.1 92.5 %all-reduce.8.cloned.1.call-start = ((), (), s32[]{:S(2)}) async-start(), calls=%async_computation.4 | async-start | bytes 262144 | tf_op jit(solution)/shard_map/while/body/eval_jaxpr/psum | solution.py:9
  684.6 56.7 %all-reduce.6.cloned.1.call-start = ((), (), s32[]{:S(2)}) async-start(), calls=%async_computation.3 | async-start | bytes 262144 | tf_op jit(solution)/shard_map/while/body/eval_jaxpr/psum | solution.py:64
  686.4 92.2 %all-reduce.8.cloned.1.call-start = ((), (), s32[]{:S(2)}) async-start(), calls=%async_computation.4 | async-start | bytes 262144 | tf_op jit(solution)/shard_map/while/body/eval_jaxpr/psum | solution.py:9
  779.6 56.7 %all-reduce.6.cloned.1.call-start = ((), (), s32[]{:S(2)}) async-start(), calls=%async_computation.3 | async-start | bytes 262144 | tf_op jit(solution)/shard_map/while/body/eval_jaxpr/psum | solution.py:64
  781.5 92.2 %all-reduce.8.cloned.1.call-start = ((), (), s32[]{:S(2)}) async-start(), calls=%async_computation.4 | async-start | bytes 262144 | tf_op jit(solution)/shard_map/while/body/eval_jaxpr/psum | solution.py:9
  874.7 0.7 copy-start
Sparse Core Ops, SparseCore 0:
  27.5 29.9 reduce-scatter.1
  60.5 52.3 all-reduce.3
  116.8 52.8 all-reduce.5
  173.0 34.0 all-reduce.7
  211.6 53.1 all-reduce.5
  268.0 34.0 all-reduce.7
  307.0 53.1 all-reduce.5
  363.4 34.0 all-reduce.7
  402.3 53.1 all-reduce.5
  458.8 34.0 all-reduce.7
  497.7 53.1 all-reduce.5
  554.1 34.0 all-reduce.7
  593.0 53.1 all-reduce.5
  649.5 34.0 all-reduce.7
  688.1 53.1 all-reduce.5
  744.6 34.0 all-reduce.7
  783.2 53.1 all-reduce.5
  839.6 34.0 all-reduce.7
where the time goes:
time: 883 us; the launch traced here: 882 us
  waiting for transfers between devices  796 us (90%)
  matrix products  39.5 us (4%)
  local copies, waits for them, and re-layouts  28 us (3%)
  between operations  13.5 us (2%)
    psum x8, waiting for transfers between devices, advance(): summed = lax.psum(partial_value, 'col')  439 us
    psum x8, waiting for transfers between devices, broadcast(): return lax.psum(jnp.where(mine, shard, jnp.zeros_like(shard)), axis)  273 us
    psum x1, waiting for transfers between devices, per_device(): permuted = lax.psum(permuted, 'col')  53.7 us
    reduce_scatter x1, waiting for transfers between devices, per_device(): lax.psum_scatter(jnp.transpose(taken.reshape(rhs_count, blocks_here * lax...  30.1 us
    dot_general x8, matrix products, apply_inverse(): lax.dot_general(values, block_inv, (((1,), (1,)), ((), ())), precision=la...  25.1 us
  transfers between devices with their start and end apart: 18, of which 18 were waited for; matrix products, arithmetic and copies ran while one was open for 0% of the time, Pallas kernels for 0%

commit v1 on v0

--- a/solution.py
+++ b/solution.py
@@ -6,7 +6,10 @@
 
 def broadcast(shard, axis, root):
     mine = lax.axis_index(axis) == root
-    return lax.psum(jnp.where(mine, shard, jnp.zeros_like(shard)), axis)
+    limits_keep_up = lambda local_values, axis_name: jnp.sum(
+        jax.lax.all_gather(local_values, axis_name), 0
+    )
+    return limits_keep_up(jnp.where(mine, shard, jnp.zeros_like(shard)), axis)
 
 
 def apply_inverse(values, block_inv):

time: 883 us -> 720 us (0.82)
  waiting for transfers between devices: 796 us -> 526 us
  blocking collectives: 0 us -> 119 us
    psum x8 -> x0, waiting for transfers between devices: 273 us -> none  [broadcast(): return lax.psum(jnp.where(mine, shard, jnp.zeros_like(shard)), axis)]
    all_gather x0 -> x8, blocking collectives: none -> 119 us  [broadcast(): jax.lax.all_gather(local_values, axis_name)]
  transfers between devices with their start and end apart: 18 -> 10, of which waited for: 18 -> 10; matrix products, arithmetic and copies ran while one was open for 0% -> 0% of each run, Pallas kernels for 0% -> 0%
where the time goes in v1:
time: 720 us; the launch traced here: 719 us
  waiting for transfers between devices  526 us (73%)
  blocking collectives  119 us (17%)
  matrix products  34.2 us (5%)
  local copies, waits for them, and re-layouts  20.8 us (3%)
  between operations  13.5 us (2%)
    psum x8, waiting for transfers between devices, advance(): summed = lax.psum(partial_value, 'col')  442 us
    all_gather x8, blocking collectives, broadcast(): jax.lax.all_gather(local_values, axis_name)  119 us
    psum x1, waiting for transfers between devices, per_device(): permuted = lax.psum(permuted, 'col')  53.7 us
    reduce_scatter x1, waiting for transfers between devices, per_device(): lax.psum_scatter(jnp.transpose(taken.reshape(rhs_count, blocks_here * lax...  30.1 us
    dot_general x8, matrix products, apply_inverse(): lax.dot_general(values, block_inv, (((1,), (1,)), ((), ())), precision=la...  19.8 us
    gather x2, local copies, waits for them, and re-layouts, per_device(): taken = jnp.take(rhs, jnp.clip(located, 0, source_len - 1), axis=1)  16.3 us
    dot_general x8, matrix products, advance(): lax.dot_general(solved.reshape(rhs_count, rounds * piece_len), block_rows...  14.4 us
  transfers between devices with their start and end apart: 10, of which 10 were waited for; matrix products, arithmetic and copies ran while one was open for 0% of the time, Pallas kernels for 0%

profile of v1, /device:TPU:0, one launch (start us, length us, event | category | flops | bytes accessed | tf_op | source)
XLA Modules:
  0.0 718.9 jit_solution(14909030762982771621)
XLA Ops:
  8.1 1.8 copy.5
  9.9 14.2 %gather_fusion = f32[4096,64]{1,0:T(8,128)} fusion(f32[64,4096]{0,1:T(8,128)S(1)} %copy.5, s32[4096]{0:T(1024)S(1)} %fusion.9), kind=kCustom, calls=%fused_computation | custom fusion | bytes 2113536 | tf_op jit(solution)/shard_map/jit(_take)/gather | solution.py:41
  24.0 2.2 copy.6
  27.5 30.1 %reduce-scatter.2.cloned.1.call-done = f32[2,64,512]{2,1,0:T(8,128)} async-done(((f32[8,64,512]{2,1,0:T(8,128)}), f32[2,64,512]{2,1,0:T(8,128)}) %reduce-scatter.2.cloned.1.call-update) | async-done | bytes 262160 | tf_op jit(solution)/shard_map/reduce_scatter | solution.py:43
  59.4 53.7 %all-reduce.3.cloned.1.call-done = f32[2,64,512]{2,1,0:T(8,128)} async-done(((f32[2,64,512]{2,1,0:T(8,128)}), f32[2,64,512]{2,1,0:T(8,128)}) %all-reduce.3.cloned.1.call-update) | async-done | bytes 262160 | tf_op jit(solution)/shard_map/psum | solution.py:51
  113.1 598.3 %while.16 = (s32[]{:T(128)}, f32[64,4,1,128]{3,2,1,0:T(1,128)S(1)}, s32[]{:T(128)}, f32[2,64,512]{2,1,0:T(8,128)}, f32[1024,512]{1,0:T(8,128)S(1)}, /*index=5*/f...) while((s32[]{:T(128)}, f32[64,4,1,128]{3,2,1,0:T(1,128)S(1)}, ...), condition=%wide.region_5.6_spmd, body=%wide.region_2.5_spmd.sunk | while | flops 402858048 | bytes 5015904 | solution.py:80
  115.1 54.8 %all-reduce.5.cloned.1.call-done = f32[64,512]{1,0:T(8,128)} async-done(((f32[64,512]{1,0:T(8,128)}), f32[64,512]{1,0:T(8,128)}) %all-reduce.5.cloned.1.call-update) | async-done | bytes 131088 | tf_op jit(solution)/shard_map/while/body/eval_jaxpr/psum | solution.py:67
  169.9 2.5 convolution_select_fusion.2
  172.3 14.9 %all-gather.2 = f32[256,512]{1,0:T(8,128)S(1)} all-gather(f32[64,512]{1,0:T(8,128)S(1)} %convolution_select_fusion.2), channel_id=2, replica_groups=mesh['row'=4,'col'=8] {'row'}, dimensions={0}, use_global_device_ids=true | all-gather | bytes 655360 | tf_op jit(solution)/shard_map/while/body/eval_jaxpr/all_gather | solution.py:10
  187.5 1.8 convolution_bitcast_fusion.2
  189.4 55.2 %all-reduce.5.cloned.1.call-done = f32[64,512]{1,0:T(8,128)} async-done(((f32[64,512]{1,0:T(8,128)}), f32[64,512]{1,0:T(8,128)}) %all-reduce.5.cloned.1.call-update) | async-done | bytes 131088 | tf_op jit(solution)/shard_map/while/body/eval_jaxpr/psum | solution.py:67
  244.6 2.5 convolution_select_fusion.2
  247.1 14.9 %all-gather.2 = f32[256,512]{1,0:T(8,128)S(1)} all-gather(f32[64,512]{1,0:T(8,128)S(1)} %convolution_select_fusion.2), channel_id=2, replica_groups=mesh['row'=4,'col'=8] {'row'}, dimensions={0}, use_global_device_ids=true | all-gather | bytes 655360 | tf_op jit(solution)/shard_map/while/body/eval_jaxpr/all_gather | solution.py:10
  264.1 55.2 %all-reduce.5.cloned.1.call-done = f32[64,512]{1,0:T(8,128)} async-done(((f32[64,512]{1,0:T(8,128)}), f32[64,512]{1,0:T(8,128)}) %all-reduce.5.cloned.1.call-update) | async-done | bytes 131088 | tf_op jit(solution)/shard_map/while/body/eval_jaxpr/psum | solution.py:67
  319.3 2.5 convolution_select_fusion.2
  321.8 14.9 %all-gather.2 = f32[256,512]{1,0:T(8,128)S(1)} all-gather(f32[64,512]{1,0:T(8,128)S(1)} %convolution_select_fusion.2), channel_id=2, replica_groups=mesh['row'=4,'col'=8] {'row'}, dimensions={0}, use_global_device_ids=true | all-gather | bytes 655360 | tf_op jit(solution)/shard_map/while/body/eval_jaxpr/all_gather | solution.py:10
  336.9 1.8 convolution_bitcast_fusion.2
  338.8 55.2 %all-reduce.5.cloned.1.call-done = f32[64,512]{1,0:T(8,128)} async-done(((f32[64,512]{1,0:T(8,128)}), f32[64,512]{1,0:T(8,128)}) %all-reduce.5.cloned.1.call-update) | async-done | bytes 131088 | tf_op jit(solution)/shard_map/while/body/eval_jaxpr/psum | solution.py:67
  394.1 2.5 convolution_select_fusion.2
  396.5 14.9 %all-gather.2 = f32[256,512]{1,0:T(8,128)S(1)} all-gather(f32[64,512]{1,0:T(8,128)S(1)} %convolution_select_fusion.2), channel_id=2, replica_groups=mesh['row'=4,'col'=8] {'row'}, dimensions={0}, use_global_device_ids=true | all-gather | bytes 655360 | tf_op jit(solution)/shard_map/while/body/eval_jaxpr/all_gather | solution.py:10
  413.6 55.5 %all-reduce.5.cloned.1.call-done = f32[64,512]{1,0:T(8,128)} async-done(((f32[64,512]{1,0:T(8,128)}), f32[64,512]{1,0:T(8,128)}) %all-reduce.5.cloned.1.call-update) | async-done | bytes 131088 | tf_op jit(solution)/shard_map/while/body/eval_jaxpr/psum | solution.py:67
  469.1 2.5 convolution_select_fusion.2
  471.6 14.9 %all-gather.2 = f32[256,512]{1,0:T(8,128)S(1)} all-gather(f32[64,512]{1,0:T(8,128)S(1)} %convolution_select_fusion.2), channel_id=2, replica_groups=mesh['row'=4,'col'=8] {'row'}, dimensions={0}, use_global_device_ids=true | all-gather | bytes 655360 | tf_op jit(solution)/shard_map/while/body/eval_jaxpr/all_gather | solution.py:10
  488.6 55.5 %all-reduce.5.cloned.1.call-done = f32[64,512]{1,0:T(8,128)} async-done(((f32[64,512]{1,0:T(8,128)}), f32[64,512]{1,0:T(8,128)}) %all-reduce.5.cloned.1.call-update) | async-done | bytes 131088 | tf_op jit(solution)/shard_map/while/body/eval_jaxpr/psum | solution.py:67
  544.1 2.5 convolution_select_fusion.2
  546.6 14.9 %all-gather.2 = f32[256,512]{1,0:T(8,128)S(1)} all-gather(f32[64,512]{1,0:T(8,128)S(1)} %convolution_select_fusion.2), channel_id=2, replica_groups=mesh['row'=4,'col'=8] {'row'}, dimensions={0}, use_global_device_ids=true | all-gather | bytes 655360 | tf_op jit(solution)/shard_map/while/body/eval_jaxpr/all_gather | solution.py:10
  563.6 55.5 %all-reduce.5.cloned.1.call-done = f32[64,512]{1,0:T(8,128)} async-done(((f32[64,512]{1,0:T(8,128)}), f32[64,512]{1,0:T(8,128)}) %all-reduce.5.cloned.1.call-update) | async-done | bytes 131088 | tf_op jit(solution)/shard_map/while/body/eval_jaxpr/psum | solution.py:67
  619.2 2.5 convolution_select_fusion.2
  621.6 14.9 %all-gather.2 = f32[256,512]{1,0:T(8,128)S(1)} all-gather(f32[64,512]{1,0:T(8,128)S(1)} %convolution_select_fusion.2), channel_id=2, replica_groups=mesh['row'=4,'col'=8] {'row'}, dimensions={0}, use_global_device_ids=true | all-gather | bytes 655360 | tf_op jit(solution)/shard_map/while/body/eval_jaxpr/all_gather | solution.py:10
  638.7 55.2 %all-reduce.5.cloned.1.call-done = f32[64,512]{1,0:T(8,128)} async-done(((f32[64,512]{1,0:T(8,128)}), f32[64,512]{1,0:T(8,128)}) %all-reduce.5.cloned.1.call-update) | async-done | bytes 131088 | tf_op jit(solution)/shard_map/while/body/eval_jaxpr/psum | solution.py:67
  693.9 2.5 convolution_select_fusion.2
  696.4 14.9 %all-gather.2 = f32[256,512]{1,0:T(8,128)S(1)} all-gather(f32[64,512]{1,0:T(8,128)S(1)} %convolution_select_fusion.2), channel_id=2, replica_groups=mesh['row'=4,'col'=8] {'row'}, dimensions={0}, use_global_device_ids=true | all-gather | bytes 655360 | tf_op jit(solution)/shard_map/while/body/eval_jaxpr/all_gather | solution.py:10
  (59 shorter events, 17.5 us)
Async XLA Ops:
  6.5 51.1 %reduce-scatter.2.cloned.1.call-start = ((), (), s32[]{:S(2)}) async-start(), calls=%async_computation.1 | async-start | bytes 1310720 | tf_op jit(solution)/shard_map/reduce_scatter | solution.py:43
  27.4 85.6 %all-reduce.3.cloned.1.call-start = ((), (), s32[]{:S(2)}) async-start(), calls=%async_computation.2 | async-start | bytes 524288 | tf_op jit(solution)/shard_map/psum | solution.py:51
  113.1 56.7 %all-reduce.5.cloned.1.call-start = ((), (), s32[]{:S(2)}) async-start(), calls=%async_computation.3 | async-start | bytes 262144 | tf_op jit(solution)/shard_map/while/body/eval_jaxpr/psum | solution.py:67
  187.4 57.2 %all-reduce.5.cloned.1.call-start = ((), (), s32[]{:S(2)}) async-start(), calls=%async_computation.3 | async-start | bytes 262144 | tf_op jit(solution)/shard_map/while/body/eval_jaxpr/psum | solution.py:67
  262.1 57.2 %all-reduce.5.cloned.1.call-start = ((), (), s32[]{:S(2)}) async-start(), calls=%async_computation.3 | async-start | bytes 262144 | tf_op jit(solution)/shard_map/while/body/eval_jaxpr/psum | solution.py:67
  336.9 57.2 %all-reduce.5.cloned.1.call-start = ((), (), s32[]{:S(2)}) async-start(), calls=%async_computation.3 | async-start | bytes 262144 | tf_op jit(solution)/shard_map/while/body/eval_jaxpr/psum | solution.py:67
  411.6 57.5 %all-reduce.5.cloned.1.call-start = ((), (), s32[]{:S(2)}) async-start(), calls=%async_computation.3 | async-start | bytes 262144 | tf_op jit(solution)/shard_map/while/body/eval_jaxpr/psum | solution.py:67
  486.7 57.5 %all-reduce.5.cloned.1.call-start = ((), (), s32[]{:S(2)}) async-start(), calls=%async_computation.3 | async-start | bytes 262144 | tf_op jit(solution)/shard_map/while/body/eval_jaxpr/psum | solution.py:67
  561.7 57.5 %all-reduce.5.cloned.1.call-start = ((), (), s32[]{:S(2)}) async-start(), calls=%async_computation.3 | async-start | bytes 262144 | tf_op jit(solution)/shard_map/while/body/eval_jaxpr/psum | solution.py:67
  636.7 57.2 %all-reduce.5.cloned.1.call-start = ((), (), s32[]{:S(2)}) async-start(), calls=%async_computation.3 | async-start | bytes 262144 | tf_op jit(solution)/shard_map/while/body/eval_jaxpr/psum | solution.py:67
  711.5 0.7 copy-start
Sparse Core Ops, SparseCore 0:
  27.6 29.9 reduce-scatter.1
  60.6 52.3 all-reduce.2
  117.0 52.8 all-reduce.4
  190.9 53.5 all-reduce.4
  265.7 53.6 all-reduce.4
  340.4 53.5 all-reduce.4
  415.5 53.5 all-reduce.4
  490.5 53.5 all-reduce.4
  565.5 53.5 all-reduce.4
  640.3 53.5 all-reduce.4
